TPU v7x, 128 devices: a 2x2x16 block of a 8x8x16 slice. The times are simulated.
128 devices in a mesh: groups: 4 (over x, y), blk: 32 (over z, core).
Axes of the slice: x: 2, y: 2, z: 16, core: 2. Of those that a mesh axis runs over, the one named last changes fastest.
The devices are a block of a 8x8x16 slice.
Arguments:
- points: bfloat16 [196608, 1024], P(('groups', 'blk')), parts along dimension 0, may hold values from -6 to 6
- coverage: float32 [196608], P(('groups', 'blk')), parts along dimension 0, may hold values from 0 to 1.5
- candidates: bfloat16 [16384, 1024], P(('groups', 'blk')), parts along dimension 0, may hold values from -6 to 6
- cand_count: int32 [128], P(('groups', 'blk')), parts along dimension 0, may hold values from 16 to 128, as said below
- acc_index: int32 [128, 16], P(('groups', 'blk')), parts along dimension 0, may hold values from 0 to 127, as said below
Outputs:
- gain_out: float32 [16384], P(('groups', 'blk')), parts along dimension 0
- new_coverage: float32 [196608], P(('groups', 'blk')), parts along dimension 0
There are 4 independent parts, one for each index of `groups`. A program takes and returns all parts, laid end to end along the dimension named above; each array names one. Nothing has to cross between parts.
Inputs may be any that keep to these rules, and one draw needn't show every extreme that they name: `cand_count`: some device has all 128 slots live. `acc_index`: each entry of row b is below cand_count[b]; entries may repeat.
All inputs are finite; a program needn't handle non-finite values.
Results may differ from a plain program's by a relative error of at most 0.0003.
Values may be sent and summed in bfloat16 or wider, within the bound.
A program may use at most 64 MiB of HBM per device.

v0:
```python
import jax
import jax.numpy as jnp
from jax import lax
from jax.sharding import Mesh
from jax.sharding import PartitionSpec as P

BLK = ("blk_0", "blk_1")
GROUPS_BLK = ("groups", "blk_0", "blk_1")


def in_blocks(shard, dim, count):
    dims = shard.shape
    parts = shard.reshape(*dims[:dim], count, dims[dim] // count, *dims[dim + 1 :])
    return jnp.moveaxis(parts, dim, 0)


def summed_on_arrival(shard, axis, dim):
    parts = in_blocks(shard, dim, lax.axis_size(axis))
    arrived = lax.all_to_all(parts, axis, split_axis=0, concat_axis=0, tiled=True)
    return arrived.sum(axis=0)


def gathered_by_axis(shard, axes, dim):
    if not axes:
        return shard
    nearer = lax.all_gather(shard, axes[-1], axis=dim, tiled=True)
    return gathered_by_axis(nearer, axes[:-1], dim)


def block_terms(points, coverage, cand_block, factor):
    similar = (
        jnp.einsum("pd,cd->pc", points, cand_block, preferred_element_type=jnp.float32) * factor
    )
    return (similar, jnp.sum(jnp.maximum(similar - coverage[:, None], 0.0), axis=0))


def per_device(points, coverage, candidates, cand_count, acc_index):
    width = points.shape[1]
    slots = candidates.shape[0]
    factor = 1.0 / jnp.sqrt(jnp.float32(width))
    devices = lax.axis_size(BLK)
    point_total = jnp.float32(points.shape[0] * devices)
    slot_ids = jnp.arange(slots, dtype=jnp.int32)
    cover = coverage
    shard_rows = lax.all_gather(candidates, BLK, axis=0, tiled=True)
    similar, sums = block_terms(points, coverage, shard_rows, factor)
    every_sum = sums
    every_sum, cover = (every_sum, cover)
    gain_sum = summed_on_arrival(every_sum, BLK, 0)
    live_rows = slot_ids < cand_count[0]
    gain_out = jnp.where(live_rows, gain_sum / point_total, 0.0)
    picked = jnp.take(candidates, acc_index[0], axis=0)
    similar = (
        jnp.einsum(
            "pd,ad->pa",
            points,
            gathered_by_axis(picked, ("blk_1", "blk_0"), 0),
            preferred_element_type=jnp.float32,
        )
        * factor
    )
    new_coverage = jnp.maximum(coverage, jnp.max(similar, axis=1))
    return (gain_out, new_coverage)


def solution(mesh):
    split = Mesh(mesh.devices.reshape(mesh.shape["groups"], 16, 2), ("groups", "blk_0", "blk_1"))
    return jax.shard_map(
        per_device,
        mesh=split,
        in_specs=(
            P(GROUPS_BLK, None),
            P(GROUPS_BLK),
            P(GROUPS_BLK, None),
            P(GROUPS_BLK),
            P(GROUPS_BLK, None),
        ),
        out_specs=(P(GROUPS_BLK), P(GROUPS_BLK)),
        check_vma=False,
    )
```

profile of v0, /device:TPU:84, one launch (start us, length us, event | category | flops | bytes accessed | tf_op | source)
XLA Modules:
  0.0 137.2 jit_solution(8278887492679083085)
XLA Ops:
  7.2 0.0 copy-start
  7.2 0.1 all-gather.3.cloned.1.call-start
  7.3 0.7 all-gather.3.cloned.1.call-update
  8.0 0.1 all-gather.5.cloned.1.call-start
  8.1 0.7 fusion.1
  8.8 1.6 %gather_fusion = bf16[16,1024]{1,0:T(8,128)(2,1)S(1)} fusion(bf16[128,1024]{1,0:T(8,128)(2,1)} %param.7, s32[1024]{0:T(1024)S(1)} %pad_clamp_fusion), kind=kCustom, calls=%fused_computation | custom fusion | bytes 65600 | tf_op jit(solution)/shard_map/jit(_take)/gather | solution.py:52
  10.4 0.7 compare_and_fusion
  11.1 0.1 broadcast_select_fusion
  11.1 46.4 %all_gather.10 = bf16[256,1024]{1,0:T(8,128)(2,1)} all-gather(bf16[16,1024]{1,0:T(8,128)(2,1)S(1)} %broadcast_select_fusion), channel_id=1, replica_groups=mesh['groups'=4,'blk_0'=16,'blk_1'=2] {'blk_0'}, dimensions={0}, use_global_device_ids=true | all-gather | bytes 557056 | tf_op jit(solution)/shard_map/all_gather | solution.py:26
  57.5 0.1 all-gather.5.cloned.1.call-update
  58.2 34.8 %all-gather.3.cloned.1.call-done = bf16[4096,1024]{1,0:T(8,128)(2,1)} async-done(((bf16[128,1024]{1,0:T(8,128)(2,1)}), bf16[4096,1024]{1,0:T(8,128)(2,1)}) %all-gather.3.cloned.1.call-update) | async-done | bytes 8388624 | tf_op jit(solution)/shard_map/all_gather | solution.py:45
  93.0 0.0 copy-done
  93.0 17.1 %maximum_reduce_fusion = f32[4096]{0:T(1024)} fusion(bf16[1536,1024]{1,0:T(8,128)(2,1)S(1)} %copy-done, bf16[4096,1024]{1,0:T(8,128)(2,1)} %all-gather.3.cloned.1.call-done, f32[1536]{0:T(1024)} %param.6), kind=kOutput, calls=%fused_computation.1 | convolution fusion | flops 12910063616 | bytes 11556864 | tf_op jit(solution)/shard_map/pd,cd->pc/dot_general | solution.py:32
  110.2 0.0 copy-start.1
  110.2 7.9 %all-to-all-start = ((f32[32,1,128]{2,1,0:T(1,128)}), f32[32,1,128]{2,1,0:T(1,128)S(1)}, u32[]{:S(2)}, u32[]{:S(2)}) async-start(f32[32,1,128]{2,1,0:T(1,128)} %bitcast.1), calls=%async_computation | async-start | bytes 32768 | tf_op jit(solution)/shard_map/all_to_all | solution.py:19
  118.0 0.0 all-gather.5.cloned.1.call-done
  118.1 3.1 %fusion = f32[1536]{0:T(1024)S(1)} fusion(bf16[512,1024]{1,0:T(8,128)(2,1)} %all-gather.5.cloned.1.call-done, bf16[1536,1024]{1,0:T(8,128)(2,1)S(1)} %copy-done), kind=kOutput, calls=%fused_computation.3 | convolution fusion | flops 1612184064 | bytes 4200448 | tf_op jit(solution)/shard_map/pd,ad->pa/dot_general | solution.py:54
  121.1 0.0 copy-done.1
  121.2 0.6 max.11
  121.8 8.1 %all-to-all-done = f32[32,1,128]{2,1,0:T(1,128)S(1)} async-done(((f32[32,1,128]{2,1,0:T(1,128)}), f32[32,1,128]{2,1,0:T(1,128)S(1)}, u32[]{:S(2)}, u32[]{:S(2)}) %all-to-all-start) | async-done | bytes 16416 | tf_op jit(solution)/shard_map/all_to_all | solution.py:19
  129.9 0.5 compare_select_fusion.2
  (2 shorter events, 0.0 us)
Async XLA Ops:
  7.2 85.9 %copy-start = (bf16[1536,1024]{1,0:T(8,128)(2,1)S(1)}, bf16[1536,1024]{1,0:T(8,128)(2,1)}, u32[]{:S(2)}) copy-start(bf16[1536,1024]{1,0:T(8,128)(2,1)} %param.5) | copy-start | bytes 9437188
  7.2 85.8 %all-gather.3.cloned.1.call-start = ((), (), s32[]{:S(2)}) async-start(), calls=%async_computation.1 | async-start | bytes 8650752 | tf_op jit(solution)/shard_map/all_gather | solution.py:45
  8.0 110.1 %all-gather.5.cloned.1.call-start = ((), (), s32[]{:S(2)}) async-start(), calls=%async_computation.2 | async-start | bytes 1572864 | tf_op jit(solution)/shard_map/all_gather | solution.py:26
  110.2 11.0 %copy-start.1 = (f32[1536]{0:T(1024)S(1)}, f32[1536]{0:T(1024)}, u32[]{:S(2)}) copy-start(f32[1536]{0:T(1024)} %param.6) | copy-start | bytes 18436
  110.2 19.7 %all-to-all-start = ((f32[32,1,128]{2,1,0:T(1,128)}), f32[32,1,128]{2,1,0:T(1,128)S(1)}, u32[]{:S(2)}, u32[]{:S(2)}) async-start(f32[32,1,128]{2,1,0:T(1,128)} %bitcast.1), calls=%async_computation | async-start | bytes 32768 | tf_op jit(solution)/shard_map/all_to_all | solution.py:19
Sparse Core Ops, SparseCore 0:
  9.7 83.2 all-gather.2
  94.7 11.6 all-gather.4
where the time goes:
time: 138 us; the launch traced here: 137 us
  blocking collectives  46.4 us (34%)
  waiting for transfers between devices  43.7 us (32%)
  matrix products  20.2 us (15%)
  between operations  14.8 us (11%)
  starting transfers between devices  8 us (6%)
  other arithmetic  2.62 us (2%)
  local copies, waits for them, and re-layouts  1.61 us (1%)
    all_gather x1, blocking collectives, gathered_by_axis(): nearer = lax.all_gather(shard, axes[-1], axis=dim, tiled=True)  46.4 us
    all_gather x1, waiting for transfers between devices, per_device(): shard_rows = lax.all_gather(candidates, BLK, axis=0, tiled=True)  34.8 us
    dot_general x1, matrix products, block_terms(): jnp.einsum('pd,cd->pc', points, cand_block, preferred_element_type=jnp.fl...  17.1 us
    all_to_all x1, waiting for transfers between devices, summed_on_arrival(): lax.all_to_all(parts, axis, split_axis=0, concat_axis=0, tiled=True)  8.09 us
    all_to_all x1, starting transfers between devices, summed_on_arrival(): lax.all_to_all(parts, axis, split_axis=0, concat_axis=0, tiled=True)  7.88 us
    dot_general x1, matrix products, per_device(): jnp.einsum('pd,ad->pa', points, gathered_by_axis(picked, ('blk_1', 'blk_0...  3.06 us
  transfers between devices with their start and end apart: 3, of which 2 were waited for; matrix products, arithmetic and copies ran while one was open for 17% of the time, Pallas kernels for 0%

commit v1 on v0

--- a/solution.py
+++ b/solution.py
@@ -42,7 +42,10 @@
     point_total = jnp.float32(points.shape[0] * devices)
     slot_ids = jnp.arange(slots, dtype=jnp.int32)
     cover = coverage
-    shard_rows = lax.all_gather(candidates, BLK, axis=0, tiled=True)
+    shard_rows = jnp.concatenate(
+        jax.lax.all_to_all(jnp.stack([candidates] * jax.lax.axis_size(BLK), axis=0), BLK, 0, 0),
+        axis=0,
+    )
     similar, sums = block_terms(points, coverage, shard_rows, factor)
     every_sum = sums
     every_sum, cover = (every_sum, cover)

time: 138 us -> 470 us (3.41)
  blocking collectives: 46.4 us -> 390 us
  waiting for transfers between devices: 43.7 us -> 8.17 us
  starting transfers between devices: 8 us -> 29.3 us
    all_gather x1, blocking collectives: 46.4 us -> 390 us  [gathered_by_axis(): nearer = lax.all_gather(shard, axes[-1], axis=dim, tiled=True)]
    all_gather x1 -> x0, waiting for transfers between devices: 34.8 us -> none  [per_device(): shard_rows = lax.all_gather(candidates, BLK, axis=0, tiled=True)]
    all_to_all x0 -> x1, starting transfers between devices: none -> 17.9 us  [per_device(): jax.lax.all_to_all(jnp.stack([candidates] * jax.lax.axis_size(BLK), axis=...]
    another operation x0 -> x1, local copies, waits for them, and re-layouts: none -> 5.4 us  [per_device(): jnp.stack([candidates] * jax.lax.axis_size(BLK), axis=0)]
  transfers between devices with their start and end apart: 3 -> 3, of which waited for: 2 -> 1; matrix products, arithmetic and copies ran while one was open for 17% -> 5% of each run, Pallas kernels for 0% -> 0%
where the time goes in v1:
time: 470 us
  blocking collectives  390 us (83%)
  starting transfers between devices  29.3 us (6%)
  matrix products  20.2 us (4%)
  between operations  14.8 us (3%)
  waiting for transfers between devices  8.17 us (2%)
  local copies, waits for them, and re-layouts  6.01 us (1%)
    all_gather x1, blocking collectives, gathered_by_axis(): nearer = lax.all_gather(shard, axes[-1], axis=dim, tiled=True)  390 us
    all_to_all x1, starting transfers between devices, per_device(): jax.lax.all_to_all(jnp.stack([candidates] * jax.lax.axis_size(BLK), axis=...  17.9 us
    dot_general x1, matrix products, block_terms(): jnp.einsum('pd,cd->pc', points, cand_block, preferred_element_type=jnp.fl...  17.2 us
    all_to_all x1, starting transfers between devices, summed_on_arrival(): lax.all_to_all(parts, axis, split_axis=0, concat_axis=0, tiled=True)  11.3 us
  transfers between devices with their start and end apart: 3, of which 1 were waited for; matrix products, arithmetic and copies ran while one was open for 5% of the time, Pallas kernels for 0%

profile of v1, /device:TPU:84, one launch (start us, length us, event | category | flops | bytes accessed | tf_op | source)
XLA Modules:
  0.0 469.6 jit_solution(15381116500284938201)
XLA Ops:
  7.2 0.0 copy-start
  7.2 5.4 %stack.2 = bf16[32,128,1024]{2,1,0:T(8,128)(2,1)} broadcast(bf16[128,1024]{1,0:T(8,128)(2,1)} %param.7), dimensions={1,2} | broadcast | bytes 8650752 | tf_op jit(solution)/shard_map/stack | solution.py:46
  12.6 0.0 copy-start.3
  12.6 0.0 copy-start.1
  12.6 0.0 copy-start.2
  12.6 17.9 %all-to-all-start = ((bf16[32,128,1024]{2,1,0:T(8,128)(2,1)}), bf16[32,128,1024]{2,1,0:T(8,128)(2,1)}, u32[]{:S(2)}, u32[]{:S(2)}) async-start(bf16[32,128,1024]{2,1,0:T(8,128)(2,1)} %stack.2), calls=%async_computation | async-start | bytes 16777216 | tf_op jit(solution)/shard_map/all_to_all | solution.py:46
  30.6 0.1 all-gather.2.cloned.1.call-start
  30.6 0.0 copy-done.3
  30.7 0.0 copy-done.1
  30.7 0.6 gather_fusion
  31.3 0.1 broadcast_select_fusion
  31.4 389.8 %all_gather.6 = bf16[256,1024]{1,0:T(8,128)(2,1)} all-gather(bf16[16,1024]{1,0:T(8,128)(2,1)S(1)} %broadcast_select_fusion), channel_id=1, replica_groups=mesh['groups'=4,'blk_0'=16,'blk_1'=2] {'blk_0'}, dimensions={0}, use_global_device_ids=true | all-gather | bytes 557056 | tf_op jit(solution)/shard_map/all_gather | solution.py:26
  421.2 0.1 all-gather.2.cloned.1.call-update
  421.9 0.0 all-to-all-done
  421.9 0.0 copy-done
  421.9 0.0 copy-done.2
  421.9 17.2 %maximum_reduce_fusion = f32[4096]{0:T(1024)} fusion(bf16[1536,1024]{1,0:T(8,128)(2,1)S(1)} %copy-done, bf16[4096,1024]{1,0:T(8,128)(2,1)} %bitcast.1, f32[1536]{0:T(1024)S(1)} %copy-done.2), kind=kOutput, calls=%fused_computation.1 | convolution fusion | flops 12910063616 | bytes 11556864 | tf_op jit(solution)/shard_map/pd,cd->pc/dot_general | solution.py:32
  439.1 11.3 %all-to-all-start.1 = ((f32[32,1,128]{2,1,0:T(1,128)}), f32[32,1,128]{2,1,0:T(1,128)S(1)}, u32[]{:S(2)}, u32[]{:S(2)}) async-start(f32[32,1,128]{2,1,0:T(1,128)} %bitcast.2), calls=%async_computation.1 | async-start | bytes 32768 | tf_op jit(solution)/shard_map/all_to_all | solution.py:19
  450.4 0.0 all-gather.2.cloned.1.call-done
  450.4 3.1 fusion
  453.5 0.6 max.11
  454.1 8.1 %all-to-all-done.1 = f32[32,1,128]{2,1,0:T(1,128)S(1)} async-done(((f32[32,1,128]{2,1,0:T(1,128)}), f32[32,1,128]{2,1,0:T(1,128)S(1)}, u32[]{:S(2)}, u32[]{:S(2)}) %all-to-all-start.1) | async-done | bytes 16416 | tf_op jit(solution)/shard_map/all_to_all | solution.py:19
  462.2 0.5 compare_select_fusion.2
  (4 shorter events, 0.0 us)
Async XLA Ops:
  7.2 414.7 %copy-start = (bf16[1536,1024]{1,0:T(8,128)(2,1)S(1)}, bf16[1536,1024]{1,0:T(8,128)(2,1)}, u32[]{:S(2)}) copy-start(bf16[1536,1024]{1,0:T(8,128)(2,1)} %param.5) | copy-start | bytes 9437188
  12.6 18.0 %copy-start.3 = (s32[1,16]{1,0:T(1,128)S(1)}, s32[1,16]{1,0:T(1,128)}, u32[]{:S(2)}) copy-start(s32[1,16]{1,0:T(1,128)} %param.9) | copy-start | bytes 196
  12.6 18.1 %copy-start.1 = (bf16[128,1024]{1,0:T(8,128)(2,1)S(1)}, bf16[128,1024]{1,0:T(8,128)(2,1)}, u32[]{:S(2)}) copy-start(bf16[128,1024]{1,0:T(8,128)(2,1)} %param.7) | copy-start | bytes 786436
  12.6 409.3 %copy-start.2 = (f32[1536]{0:T(1024)S(1)}, f32[1536]{0:T(1024)}, u32[]{:S(2)}) copy-start(f32[1536]{0:T(1024)} %param.6) | copy-start | bytes 18436
  12.6 409.3 %all-to-all-start = ((bf16[32,128,1024]{2,1,0:T(8,128)(2,1)}), bf16[32,128,1024]{2,1,0:T(8,128)(2,1)}, u32[]{:S(2)}, u32[]{:S(2)}) async-start(bf16[32,128,1024]{2,1,0:T(8,128)(2,1)} %stack.2), calls=%async_computation | async-start | bytes 16777216 | tf_op jit(solution)/shard_map/all_to_all | solution.py:46
  30.6 419.9 %all-gather.2.cloned.1.call-start = ((), (), s32[]{:S(2)}) async-start(), calls=%async_computation.2 | async-start | bytes 1572864 | tf_op jit(solution)/shard_map/all_gather | solution.py:26
  439.1 23.1 %all-to-all-start.1 = ((f32[32,1,128]{2,1,0:T(1,128)}), f32[32,1,128]{2,1,0:T(1,128)S(1)}, u32[]{:S(2)}, u32[]{:S(2)}) async-start(f32[32,1,128]{2,1,0:T(1,128)} %bitcast.2), calls=%async_computation.1 | async-start | bytes 32768 | tf_op jit(solution)/shard_map/all_to_all | solution.py:19
Sparse Core Ops, SparseCore 0:
  421.4 16.0 all-gather.1
